TPU v7x, 256 devices: a whole 4x4x8 slice. The times are simulated.
256 devices in a mesh: cohort: 8 (over z_lo, core), gene: 32 (over x, y, z_hi).
Axes of the slice: x: 4, y: 4, z: 8 (z_hi: 2, z_lo: 4; z = z_hi * 4 + z_lo), core: 2. Of those that a mesh axis runs over, the one named last changes fastest.
Arguments:
- expression: bfloat16 [24000, 3200], P('gene'), as said below
- sample_index: int32 [8, 400], P('cohort'), may hold values from 0 to 3199, as said below
- gene_block: int32 [24000], P('gene'), may hold values from 0 to 127
Outputs:
- connectivity: float32 [4864, 128], P(('cohort', 'gene'))
Inputs may be any that keep to these rules, and one draw needn't show every extreme that they name: `sample_index`: the entries together are a permutation of the 3200 pooled samples, 400 in each cohort. Finite expression values; genes of a module co-vary with a strength that differs between cohorts.
All inputs are finite; a program needn't handle non-finite values.
Results may differ from a plain program's by a relative error of at most 0.00097.
Values may be sent and summed in bfloat16 or wider, within the bound.
No kernel may reach another device: no remote copies, remote signals or barrier semaphores. Data moves between devices by JAX's collectives and lax.ppermute only.
A program may use at most 64 MiB of HBM per device.

v0:
```python
import functools

import jax
import jax.numpy as jnp
from jax import lax
from jax.experimental import pallas as pl
from jax.experimental.pallas import tpu as pltpu
from jax.sharding import Mesh
from jax.sharding import PartitionSpec as P


MODULES = 128
ROW_DEV = 152
COHORTS = 8
SAMPLES = 400
POOL = COHORTS * SAMPLES
GENES = 750
ROWS = 19
SLOT = 24
LANES = 128
DEPTH = 512
PITCH = POOL + 4
SHORT = SAMPLES + 4
CHUNK = 640
GENE_BLOCKS = 6
COHORT_AXES = ("z_lo", "core")
GENE_AXES = ("x", "y", "z_hi")
ALL_AXES = COHORT_AXES + GENE_AXES
F32 = jnp.float32
BF16 = jnp.bfloat16


def transpose_in(load, blocks, turned):
    def chunk(i, _):
        for k in range(CHUNK // LANES):
            lane = pl.multiple_of(i * CHUNK, LANES) + k * LANES
            for b in range(blocks):
                turned[pl.ds(b * PITCH + lane, LANES), :] = load(b, lane).T
        return _

    lax.fori_loop(0, POOL // CHUNK, chunk, 0)


def gather_cohort(source, turned, grouped, blocks):
    for u in range(SAMPLES):
        sample = source[0][source[1], u]
        grouped[pl.ds(u, blocks, stride=SHORT), :] = turned[pl.ds(sample, blocks, stride=PITCH), :]


def in_turn(order, turned, groups, blocks, finish):
    gather_cohort(order[0], turned, groups[0], blocks)
    for c in range(COHORTS):
        if c + 1 < COHORTS:
            gather_cohort(order[c + 1], turned, groups[(c + 1) % 2], blocks)
        finish(c, c % 2)


def standardized(grouped, block):
    x = grouped[block * SHORT : block * SHORT + SAMPLES, :]
    centred = x - jnp.sum(x, axis=0, keepdims=True) * (1.0 / SAMPLES)
    spread = jnp.sqrt(jnp.sum(centred * centred, axis=0, keepdims=True) + 0.01 * SAMPLES)
    return centred * (1.0 / spread)


def order_of(refs):
    return [(ref, row) for ref in refs for row in range(2)]


def gene_kernel(*refs):
    lists, (x_hbm, z_ref, x_ref, turned, even, odd, arrive) = refs[:4], refs[4:]

    def fetch(i):
        lanes = pl.ds(pl.multiple_of(i * CHUNK, LANES), CHUNK)
        return pltpu.make_async_copy(x_hbm.at[:, lanes], x_ref.at[:, lanes], arrive.at[i])

    for i in range(POOL // CHUNK):
        fetch(i).start()

    def chunk(i, _):
        fetch(i).wait()
        for k in range(CHUNK // LANES):
            lane = pl.multiple_of(i * CHUNK, LANES) + k * LANES
            for b in range(GENE_BLOCKS):
                rows = min(LANES, GENES - b * LANES)
                tile = x_ref[b * LANES : b * LANES + rows, pl.ds(lane, LANES)].astype(F32)
                if rows < LANES:
                    tile = jnp.concatenate([tile, jnp.zeros((LANES - rows, LANES), F32)], axis=0)
                turned[pl.ds(b * PITCH + lane, LANES), :] = tile.T
        return _

    lax.fori_loop(0, POOL // CHUNK, chunk, 0)

    def finish(c, slot):
        for b in range(GENE_BLOCKS):
            z = standardized((even, odd)[slot], b)
            z = jnp.concatenate([z, jnp.zeros((DEPTH - SAMPLES, LANES), F32)], axis=0).astype(BF16)
            z_ref[c, b * LANES : (b + 1) * LANES, :] = z.T

    in_turn(order_of(lists), turned, (even, odd), GENE_BLOCKS, finish)


def genes(lists, x):
    return pl.pallas_call(
        gene_kernel,
        out_shape=jax.ShapeDtypeStruct((COHORTS, GENE_BLOCKS * LANES, DEPTH), BF16),
        in_specs=[pl.BlockSpec(memory_space=pltpu.SMEM)] * 4 + [pl.BlockSpec(memory_space=pltpu.HBM)],
        out_specs=pl.BlockSpec(memory_space=pltpu.VMEM),
        scratch_shapes=[
            pltpu.VMEM((GENES, POOL), BF16),
            pltpu.VMEM((GENE_BLOCKS * PITCH, LANES), F32),
            pltpu.VMEM((GENE_BLOCKS * SHORT, LANES), F32),
            pltpu.VMEM((GENE_BLOCKS * SHORT, LANES), F32),
            pltpu.SemaphoreType.DMA((POOL // CHUNK,)),
        ],
        compiler_params=pltpu.CompilerParams(vmem_limit_bytes=26 * 2**20),
        name="genes",
    )(*lists, x)


def share_of(cohort, x, y):
    return lax.rem(cohort + x * 2 + y // 2, COHORTS)


def pick_kernel(x_hbm, near_ref, mine_ref, theirs_ref, x_ref, arrive):
    copy = pltpu.make_async_copy(x_hbm.at[pl.ds(0, ROW_DEV), :], x_ref, arrive)
    copy.start()
    z_lo, core = lax.axis_index("z_lo"), lax.axis_index("core")
    x, y = lax.axis_index("x"), lax.axis_index("y")
    own = share_of(z_lo * 2 + core, x, y) * ROWS
    other = share_of((3 - z_lo) * 2 + core, x, y) * ROWS
    row = lax.broadcasted_iota(jnp.int32, (64, ROW_DEV), 0)
    column = lax.broadcasted_iota(jnp.int32, (64, ROW_DEV), 1)
    wanted = jnp.where(
        row < 19, own + row, jnp.where((row >= 43) & (row < 62), other + row - 43, -1)
    )
    select = jnp.where(column == wanted, 1.0, 0.0).astype(BF16)
    copy.wait()
    rows = jnp.dot(select, x_ref[...], preferred_element_type=F32).astype(BF16)
    near_ref[...] = rows[:16]
    mine_ref[...] = rows[16:40]
    theirs_ref[...] = rows[40:]


def pick(x):
    return pl.pallas_call(
        pick_kernel,
        out_shape=[jax.ShapeDtypeStruct((rows, POOL), BF16) for rows in (16, 24, 24)],
        in_specs=[pl.BlockSpec(memory_space=pltpu.HBM)],
        out_specs=[pl.BlockSpec(memory_space=pltpu.VMEM)] * 3,
        scratch_shapes=[pltpu.VMEM((ROW_DEV, POOL), BF16), pltpu.SemaphoreType.DMA(())],
        compiler_params=pltpu.CompilerParams(vmem_limit_bytes=6 * 2**20),
        name="pick",
    )(x)


def window_kernel(units, spots, done, *refs):
    lists, (module_ref, z_ref), refs = refs[:4], refs[4:6], refs[6:]
    before, parts, refs = refs[: len(done)], refs[len(done) : len(done) + units], refs[len(done) + units :]
    out_ref, turned, even, odd, zw0, zw1, low, consensus, label, raw = refs
    total = low.shape[1]
    blocks = total // LANES
    strips = [(p, j, r) for p in parts for j in range(p.shape[0]) for r in range(0, p.shape[1], 8)]

    def load(b, lane):
        mine = strips[b * 16 : (b + 1) * 16]
        tiles = [p[j, r : r + 8, pl.ds(lane, LANES)].astype(F32) for p, j, r in mine]
        return jnp.concatenate(tiles + [jnp.zeros((8, LANES), F32)] * (16 - len(mine)), axis=0)

    transpose_in(load, blocks, turned)
    for zw in (zw0, zw1):
        zw[SAMPLES:, :] = jnp.zeros((DEPTH - SAMPLES, total), BF16)

    def finish(c, slot):
        zw = (zw0, zw1)[slot]
        for b in range(blocks):
            zw[:SAMPLES, b * LANES : (b + 1) * LANES] = standardized((even, odd)[slot], b).astype(BF16)
        corr = jnp.dot(z_ref[c], zw[...], preferred_element_type=F32)
        low[...] = jnp.minimum(low[...], corr) if c else corr

    in_turn(order_of(lists), turned, (even, odd), blocks, finish)

    base = (1.0 + jnp.maximum(low[...], -1.0)) * 0.5
    square = base * base
    fourth = square * square
    consensus[...] = (fourth * fourth * fourth).astype(BF16)
    label[...] = jnp.full(label.shape, -1, jnp.int32)
    label[:, :GENES] = module_ref[...]
    module = lax.broadcasted_iota(jnp.int32, (MODULES, GENE_BLOCKS * LANES), 0)
    onehot = jnp.where(label[...] == module, 1.0, 0.0).astype(BF16)
    degree = jnp.dot(onehot, consensus[...], preferred_element_type=F32).T
    if not done:
        out_ref[...] = degree
        return
    raw[...] = degree
    deal([*before, raw], [*done, spots], out_ref)


def deal(sums, spots, out_ref):
    x, y, z_hi = (lax.axis_index(axis) for axis in GENE_AXES)
    cohort = lax.axis_index("z_lo") * 2 + lax.axis_index("core")
    for ref, units in zip(sums, spots, strict=True):
        for row, rows, dx, dy in units:
            from_x, from_y = lax.rem(x + dx + 4, 4), lax.rem(y + dy + 4, 4)
            share = share_of(cohort, from_x, from_y)
            half = (from_y % 2) * 2
            own = (half + z_hi) * 4 + share // 2
            other = (half + 1 - z_hi) * 4 + share // 2
            at = pl.multiple_of((share % 2) * SLOT, 8)
            if rows == 16:
                out_ref[own, pl.ds(at, 16), :] = ref[row : row + 16, :]
            else:
                out_ref[own, pl.ds(at + 16, 3), :] = ref[row : row + 3, :]
                out_ref[other, pl.ds(at, ROWS), :] = ref[row + 3 : row + 3 + ROWS, :]


def windows(lists, module, z, parts, spots, done=(), sums=()):
    total = -(-sum(p.shape[0] * p.shape[1] for p in parts) // LANES) * LANES
    blocks = total // LANES
    shape = (16, 2 * SLOT, MODULES) if done else (total, MODULES)
    return pl.pallas_call(
        functools.partial(window_kernel, len(parts), spots, done),
        out_shape=jax.ShapeDtypeStruct(shape, F32),
        in_specs=[pl.BlockSpec(memory_space=pltpu.SMEM)] * 4
        + [pl.BlockSpec(memory_space=pltpu.VMEM)] * (2 + len(sums) + len(parts)),
        out_specs=pl.BlockSpec(memory_space=pltpu.VMEM),
        scratch_shapes=[
            pltpu.VMEM((blocks * PITCH, LANES), F32),
            pltpu.VMEM((blocks * SHORT, LANES), F32),
            pltpu.VMEM((blocks * SHORT, LANES), F32),
            pltpu.VMEM((DEPTH, total), BF16),
            pltpu.VMEM((DEPTH, total), BF16),
            pltpu.VMEM((GENE_BLOCKS * LANES, total), F32),
            pltpu.VMEM((GENE_BLOCKS * LANES, total), BF16),
            pltpu.VMEM((1, GENE_BLOCKS * LANES), jnp.int32),
            pltpu.VMEM((total, MODULES), F32),
        ],
        compiler_params=pltpu.CompilerParams(vmem_limit_bytes=20 * 2**20),
    )(*lists, module, z, *sums, *parts)


def shifted(array, axis, by):
    n = lax.axis_size(axis)
    return lax.ppermute(array, axis, [(i, (i + by) % n) for i in range(n)])


def gathered(unit, first, second):
    line = [unit] + [shifted(unit, first, by) for by in (1, 3, 2)]
    stack = jnp.stack(line)
    ahead, behind = shifted(stack, second, 1), shifted(stack, second, 3)
    far = [shifted(ahead[:2], second, 1), shifted(behind[2:], second, 3)]
    one = (0, -1, 1, 2)
    where = [[(a, 0) for a in one], [(a, -1) for a in one], [(a, 1) for a in one]]
    where += [[(a, 2) for a in one[:2]], [(a, 2) for a in one[2:]]]
    if first == "y":
        where = [[(b, a) for a, b in many] for many in where]
    return list(zip([stack, ahead, behind, *far], where, strict=True))


def laid(parts):
    spots, row = [], 0
    for array, where in parts:
        for dx, dy in where:
            spots.append((row, array.shape[1], dx, dy))
            row += array.shape[1]
    return [array for array, _ in parts], tuple(spots)


def in_plane(expression, sample_index, gene_block):
    own, mine, theirs = pick(expression)
    both = jnp.concatenate([sample_index, lax.ppermute(sample_index, "core", [(0, 1), (1, 0)])])
    pairs = [(z * 2 + h, (3 - z) * 2 + 1 - h) for z in range(4) for h in range(2)]
    across = lax.ppermute(theirs, ("z_lo", "z_hi"), pairs)
    lists = [both] + [shifted(both, "z_lo", by) for by in (1, 2, 3)]

    near = gathered(own, "x", "y")
    far = gathered(mine + across, "y", "x")
    z = genes(lists, expression)
    module = gene_block.reshape(1, GENES)

    parts, spots_0 = laid(near[:3] + far[:1])
    sums_0 = windows(lists, module, z, parts, spots_0)
    parts, spots_1 = laid(near[3:] + far[1:3])
    sums_1 = windows(lists, module, z, parts, spots_1)
    parts, spots_2 = laid(far[3:])
    dealt = windows(lists, module, z, parts, spots_2, (spots_0, spots_1), (sums_0, sums_1))

    arrived = lax.all_to_all(dealt, ("x", "y"), 0, 0, tiled=True).sum(axis=0)
    arrived = arrived.reshape(2, SLOT, MODULES)[:, :ROWS]
    z_hi = lax.axis_index("z_hi")
    first = lax.ppermute(lax.dynamic_index_in_dim(arrived, z_hi, 0, False), ALL_AXES, home(0))
    second = lax.ppermute(lax.dynamic_index_in_dim(arrived, 1 - z_hi, 0, False), ALL_AXES, home(1))
    return jnp.log1p(first + second)


def home(flip):
    pairs = []
    for c in range(COHORTS):
        for x in range(4):
            for y in range(4):
                for z_hi in range(2):
                    slot = z_hi ^ flip
                    there = (2 * y + slot - c) % COHORTS
                    pairs.append((c * 32 + (x * 4 + y) * 2 + z_hi, there * 32 + (x * 4 + y) * 2 + slot))
    return pairs


def solution(mesh):
    finer = Mesh(mesh.devices.reshape(4, 2, 4, 4, 2), ALL_AXES)
    placed = (P(GENE_AXES, None), P(COHORT_AXES, None), P(GENE_AXES))
    return jax.shard_map(in_plane, mesh=finer, in_specs=placed, out_specs=P(ALL_AXES, None), check_vma=False)
```

profile of v0, /device:TPU:1, one launch (start us, length us, event | category | flops | bytes accessed | tf_op | source)
XLA Modules:
  0.0 115.8 jit_solution(188852353931625355)
XLA Ops:
  0.0 2.4 %copy-done = bf16[750,3200]{1,0:T(8,128)(2,1)S(1)} copy-done((bf16[750,3200]{1,0:T(8,128)(2,1)S(1)}, bf16[750,3200]{1,0:T(8,128)(2,1)}, u32[]{:S(2)}) %copy-start) | copy-done | bytes 4800024
  2.4 0.6 pick.1
  3.0 6.5 %collective-permute-start.9 = (bf16[24,3200]{1,0:T(8,128)(2,1)S(1)}, bf16[24,3200]{1,0:T(8,128)(2,1)S(1)}, u32[]{:S(2)}, u32[]{:S(2)}) collective-permute-start(bf16[24,3200]{1,0:T(8,128)(2,1)S(1)} %get-tuple-element.10), channel_id=1, source_target_pairs={{0,193},{1,192},{64,129},{65,128},{128,65},{129,64},{192,1},{193,0... | collective-permute-start | bytes 460808 | tf_op jit(solution)/shard_map/ppermute | solution.py:272
  9.5 7.3 %collective-permute-done.9 = bf16[24,3200]{1,0:T(8,128)(2,1)S(1)} collective-permute-done((bf16[24,3200]{1,0:T(8,128)(2,1)S(1)}, bf16[24,3200]{1,0:T(8,128)(2,1)S(1)}, u32[]{:S(2)}, u32[]{:S(2)}) %collective-permute-start.9) | collective-permute-done | bytes 153632 | tf_op jit(solution)/shard_map/ppermute | solution.py:272
  16.8 3.0 %collective-permute-start.12 = (bf16[24,3200]{1,0:T(8,128)(2,1)S(1)}, bf16[24,3200]{1,0:T(8,128)(2,1)S(1)}, u32[]{:S(2)}, u32[]{:S(2)}) collective-permute-start(bf16[24,3200]{1,0:T(8,128)(2,1)S(1)} %add.14), channel_id=1, source_target_pairs={{0,4},{2,6},{4,0},{6,2},{1,5},{3,7},{5,1},{7,3},{8,12},{10,14},{12... | collective-permute-start | bytes 460808 | tf_op jit(solution)/shard_map/ppermute | solution.py:243
  19.8 0.8 collective-permute-start.11
  20.6 0.7 collective-permute-start.10
  21.3 2.8 %collective-permute-start.6 = (bf16[16,3200]{1,0:T(8,128)(2,1)S(1)}, bf16[16,3200]{1,0:T(8,128)(2,1)S(1)}, u32[]{:S(2)}, u32[]{:S(2)}) collective-permute-start(bf16[16,3200]{1,0:T(8,128)(2,1)S(1)} %get-tuple-element.8), channel_id=1, source_target_pairs={{0,16},{8,24},{16,0},{24,8},{1,17},{9,25},{17,1},{25,9},{2,18},{10... | collective-permute-start | bytes 307208 | tf_op jit(solution)/shard_map/ppermute | solution.py:243
  24.0 0.9 collective-permute-start.5
  25.5 1.3 %collective-permute-done.11 = bf16[24,3200]{1,0:T(8,128)(2,1)S(1)} collective-permute-done((bf16[24,3200]{1,0:T(8,128)(2,1)S(1)}, bf16[24,3200]{1,0:T(8,128)(2,1)S(1)}, u32[]{:S(2)}, u32[]{:S(2)}) %collective-permute-start.11) | collective-permute-done | bytes 153632 | tf_op jit(solution)/shard_map/ppermute | solution.py:243
  27.0 1.3 %collective-permute-start.15 = (bf16[4,24,3200]{2,1,0:T(8,128)(2,1)S(1)}, bf16[4,24,3200]{2,1,0:T(8,128)(2,1)S(1)}, u32[]{:S(2)}, u32[]{:S(2)}) collective-permute-start(bf16[4,24,3200]{2,1,0:T(8,128)(2,1)S(1)} %pad_maximum_fusion.refs_9_), channel_id=1, source_target_pairs={{0,8},{8,16},{16,24},{24,0},{1,9},{9,17},{17,25},{25,1},{2,10},{10... | collective-permute-start | bytes 1843208 | tf_op jit(solution)/shard_map/ppermute | solution.py:243
  28.3 1.5 %collective-permute-start.16 = (bf16[4,24,3200]{2,1,0:T(8,128)(2,1)S(1)}, bf16[4,24,3200]{2,1,0:T(8,128)(2,1)S(1)}, u32[]{:S(2)}, u32[]{:S(2)}) collective-permute-start(bf16[4,24,3200]{2,1,0:T(8,128)(2,1)S(1)} %pad_maximum_fusion.refs_9_), channel_id=1, source_target_pairs={{0,24},{8,0},{16,8},{24,16},{1,25},{9,1},{17,9},{25,17},{2,26},{10... | collective-permute-start | bytes 1843208 | tf_op jit(solution)/shard_map/ppermute | solution.py:243
  30.2 1.7 %collective-permute-start.7 = (bf16[4,16,3200]{2,1,0:T(8,128)(2,1)S(1)}, bf16[4,16,3200]{2,1,0:T(8,128)(2,1)S(1)}, u32[]{:S(2)}, u32[]{:S(2)}) collective-permute-start(bf16[4,16,3200]{2,1,0:T(8,128)(2,1)S(1)} %pad_maximum_fusion.1.refs_6_), channel_id=1, source_target_pairs={{0,2},{2,4},{4,6},{6,0},{1,3},{3,5},{5,7},{7,1},{8,10},{10,12},{12... | collective-permute-start | bytes 1228808 | tf_op jit(solution)/shard_map/ppermute | solution.py:243
  31.9 1.4 %collective-permute-start.8 = (bf16[4,16,3200]{2,1,0:T(8,128)(2,1)S(1)}, bf16[4,16,3200]{2,1,0:T(8,128)(2,1)S(1)}, u32[]{:S(2)}, u32[]{:S(2)}) collective-permute-start(bf16[4,16,3200]{2,1,0:T(8,128)(2,1)S(1)} %pad_maximum_fusion.1.refs_6_), channel_id=1, source_target_pairs={{0,6},{2,0},{4,2},{6,4},{1,7},{3,1},{5,3},{7,5},{8,14},{10,8},{12,... | collective-permute-start | bytes 1228808 | tf_op jit(solution)/shard_map/ppermute | solution.py:243
  33.3 10.3 %collective-permute-done.15.refs_8_ = bf16[4,24,3200]{2,1,0:T(8,128)(2,1)S(1)} collective-permute-done((bf16[4,24,3200]{2,1,0:T(8,128)(2,1)S(1)}, bf16[4,24,3200]{2,1,0:T(8,128)(2,1)S(1)}, u32[]{:S(2)}, u32[]{:S(2)}) %collective-permute-start.15) | collective-permute-done | bytes 614432 | tf_op jit(solution)/shard_map/ppermute | solution.py:243
  44.2 2.2 %collective-permute-start.18 = (bf16[2,24,3200]{2,1,0:T(8,128)(2,1)S(1)}, bf16[2,24,3200]{2,1,0:T(8,128)(2,1)S(1)}, u32[]{:S(2)}, u32[]{:S(2)}) collective-permute-start(bf16[2,24,3200]{2,1,0:T(8,128)(2,1)S(1)} %slice.23), channel_id=1, source_target_pairs={{0,24},{8,0},{16,8},{24,16},{1,25},{9,1},{17,9},{25,17},{2,26},{10... | collective-permute-start | bytes 921608 | tf_op jit(solution)/shard_map/ppermute | solution.py:243
  46.5 1.9 %collective-permute-start.13 = (bf16[2,16,3200]{2,1,0:T(8,128)(2,1)S(1)}, bf16[2,16,3200]{2,1,0:T(8,128)(2,1)S(1)}, u32[]{:S(2)}, u32[]{:S(2)}) collective-permute-start(bf16[2,16,3200]{2,1,0:T(8,128)(2,1)S(1)} %slice.20), channel_id=1, source_target_pairs={{0,2},{2,4},{4,6},{6,0},{1,3},{3,5},{5,7},{7,1},{8,10},{10,12},{12... | collective-permute-start | bytes 614408 | tf_op jit(solution)/shard_map/ppermute | solution.py:243
  48.4 1.9 %collective-permute-start.14 = (bf16[2,16,3200]{2,1,0:T(8,128)(2,1)S(1)}, bf16[2,16,3200]{2,1,0:T(8,128)(2,1)S(1)}, u32[]{:S(2)}, u32[]{:S(2)}) collective-permute-start(bf16[2,16,3200]{2,1,0:T(8,128)(2,1)S(1)} %slice.21), channel_id=1, source_target_pairs={{0,6},{2,0},{4,2},{6,4},{1,7},{3,1},{5,3},{7,5},{8,14},{10,8},{12,... | collective-permute-start | bytes 614408 | tf_op jit(solution)/shard_map/ppermute | solution.py:243
  50.3 2.3 %collective-permute-start = (s32[1,400]{1,0:T(1,128)S(1)}, s32[1,400]{1,0:T(1,128)S(1)}, u32[]{:S(2)}, u32[]{:S(2)}) collective-permute-start(s32[1,400]{1,0:T(1,128)S(1)} %copy-done.3), channel_id=1, source_target_pairs={{0,32},{32,0},{1,33},{33,1},{2,34},{34,2},{3,35},{35,3},{4,36},{36... | collective-permute-start | bytes 4808 | tf_op jit(solution)/shard_map/ppermute | solution.py:270
  52.6 0.8 collective-permute-done
  53.7 4.2 %collective-permute-done.1.refs_1_ = s32[2,400]{1,0:T(2,128)S(1)} collective-permute-done((s32[2,400]{1,0:T(2,128)S(1)}, s32[2,400]{1,0:T(2,128)S(1)}, u32[]{:S(2)}, u32[]{:S(2)}) %collective-permute-start.1) | collective-permute-done | bytes 3232 | tf_op jit(solution)/shard_map/ppermute | solution.py:243
  57.9 3.4 %collective-permute-done.2.refs_2_ = s32[2,400]{1,0:T(2,128)S(1)} collective-permute-done((s32[2,400]{1,0:T(2,128)S(1)}, s32[2,400]{1,0:T(2,128)S(1)}, u32[]{:S(2)}, u32[]{:S(2)}) %collective-permute-start.2) | collective-permute-done | bytes 3232 | tf_op jit(solution)/shard_map/ppermute | solution.py:243
  61.3 2.4 %collective-permute-done.3.refs_3_ = s32[2,400]{1,0:T(2,128)S(1)} collective-permute-done((s32[2,400]{1,0:T(2,128)S(1)}, s32[2,400]{1,0:T(2,128)S(1)}, u32[]{:S(2)}, u32[]{:S(2)}) %collective-permute-start.3) | collective-permute-done | bytes 3232 | tf_op jit(solution)/shard_map/ppermute | solution.py:243
  63.7 7.7 %genes.1.refs_5_ = bf16[8,768,512]{2,1,0:T(8,128)(2,1)S(1)} custom-call(s32[2,400]{1,0:T(2,128)S(1)} %pad_add_fusion.refs_0_, s32[2,400]{1,0:T(2,128)S(1)} %collective-permute-done.1.refs_1_, s32[2,400]{1,0:T(2,128)S(1)} %collective-permute-done.2.refs_2_, s32[2,400]{1,0:T(2,128)S(1)} %collective-permute-done.3.refs_3_, bf16[750,3200]{1,0:T(8,128)(2,1)S(1)} %copy-done.1), custom_call_target="tpu_custom_call" | custom-call | tf_op jit(solution)/shard_map/genes/pallas_call | solution.py:103
  71.4 8.1 %shard_map.37.refs_6_ = f32[384,128]{1,0:T(8,128)S(1)} custom-call(s32[2,400]{1,0:T(2,128)S(1)} %pad_add_fusion.refs_0_, s32[2,400]{1,0:T(2,128)S(1)} %collective-permute-done.1.refs_1_, s32[2,400]{1,0:T(2,128)S(1)} %collective-permute-done.2.refs_2_, s32[2,400]{1,0:T(2,128)S(1)} %collective-permute-done.3.refs_3_, s32[1,750]{1,0:T(1,128)S(1)} %reshape.6.refs_4_, ...), custom_call_target="tpu_custom_call" | custom-call | tf_op jit(solution)/shard_map/pallas_call | solution.py:220
  79.6 6.6 %shard_map.38.refs_7_ = f32[256,128]{1,0:T(8,128)S(1)} custom-call(s32[2,400]{1,0:T(2,128)S(1)} %pad_add_fusion.refs_0_, s32[2,400]{1,0:T(2,128)S(1)} %collective-permute-done.1.refs_1_, s32[2,400]{1,0:T(2,128)S(1)} %collective-permute-done.2.refs_2_, s32[2,400]{1,0:T(2,128)S(1)} %collective-permute-done.3.refs_3_, s32[1,750]{1,0:T(1,128)S(1)} %reshape.6.refs_4_, ...), custom_call_target="tpu_custom_call" | custom-call | tf_op jit(solution)/shard_map/pallas_call | solution.py:220
  86.2 6.5 %shard_map.39 = f32[16,48,128]{2,1,0:T(8,128)} custom-call(s32[2,400]{1,0:T(2,128)S(1)} %pad_add_fusion.refs_0_, s32[2,400]{1,0:T(2,128)S(1)} %collective-permute-done.1.refs_1_, s32[2,400]{1,0:T(2,128)S(1)} %collective-permute-done.2.refs_2_, s32[2,400]{1,0:T(2,128)S(1)} %collective-permute-done.3.refs_3_, s32[1,750]{1,0:T(1,128)S(1)} %reshape.6.refs_4_, ...), custom_call_target="tpu_custom_call" | custom-call | tf_op jit(solution)/shard_map/pallas_call | solution.py:220
  92.7 3.6 %all-to-all-start = ((f32[16,48,128]{2,1,0:T(8,128)}), f32[16,48,128]{2,1,0:T(8,128)S(1)}, u32[]{:S(2)}, u32[]{:S(2)}) async-start(f32[16,48,128]{2,1,0:T(8,128)} %shard_map.39), calls=%async_computation | async-start | bytes 786432 | tf_op jit(solution)/shard_map/all_to_all | solution.py:287
  96.3 7.9 %all-to-all-done = f32[16,48,128]{2,1,0:T(8,128)S(1)} async-done(((f32[16,48,128]{2,1,0:T(8,128)}), f32[16,48,128]{2,1,0:T(8,128)S(1)}, u32[]{:S(2)}, u32[]{:S(2)}) %all-to-all-start) | async-done | bytes 393248 | tf_op jit(solution)/shard_map/all_to_all | solution.py:287
  104.2 3.8 %collective-permute-start.19 = (f32[19,128]{1,0:T(8,128)S(1)}, f32[19,128]{1,0:T(8,128)S(1)}, u32[]{:S(2)}, u32[]{:S(2)}) collective-permute-start(f32[19,128]{1,0:T(8,128)S(1)} %get-tuple-element.12), channel_id=1, source_target_pairs={{0,0},{1,33},{2,66},{3,99},{4,132},{5,165},{6,198},{7,231},{8,8},{... | collective-permute-start | bytes 29192 | tf_op jit(solution)/shard_map/ppermute | solution.py:290
  108.0 6.4 %collective-permute-start.20 = (f32[19,128]{1,0:T(8,128)S(1)}, f32[19,128]{1,0:T(8,128)S(1)}, u32[]{:S(2)}, u32[]{:S(2)}) collective-permute-start(f32[19,128]{1,0:T(8,128)S(1)} %get-tuple-element.11), channel_id=1, source_target_pairs={{0,33},{1,0},{2,99},{3,66},{4,165},{5,132},{6,231},{7,198},{8,41},... | collective-permute-start | bytes 29192 | tf_op jit(solution)/shard_map/ppermute | solution.py:291
  114.3 0.8 collective-permute-done.20
  (37 shorter events, 2.9 us)
Async XLA Ops:
  0.0 2.4 %copy-start = (bf16[750,3200]{1,0:T(8,128)(2,1)S(1)}, bf16[750,3200]{1,0:T(8,128)(2,1)}, u32[]{:S(2)}) copy-start(bf16[750,3200]{1,0:T(8,128)(2,1)} %x_hbm.1) | copy-start | bytes 14400004
  2.4 47.9 %copy-start.3 = (s32[1,400]{1,0:T(1,128)S(1)}, s32[1,400]{1,0:T(1,128)}, u32[]{:S(2)}) copy-start(s32[1,400]{1,0:T(1,128)} %param.4) | copy-start | bytes 4804
  2.4 58.9 %copy-start.2 = (s32[750]{0:T(1024)S(1)}, s32[750]{0:T(1024)}, u32[]{:S(2)}) copy-start(s32[750]{0:T(1024)} %param.5) | copy-start | bytes 9004
  2.4 61.3 %copy-start.1 = (bf16[750,3200]{1,0:T(8,128)(2,1)S(1)}, bf16[750,3200]{1,0:T(8,128)(2,1)}, u32[]{:S(2)}) copy-start(bf16[750,3200]{1,0:T(8,128)(2,1)} %x_hbm.1) | copy-start | bytes 14400004
  3.0 13.8 %collective-permute-start.9 = (bf16[24,3200]{1,0:T(8,128)(2,1)S(1)}, bf16[24,3200]{1,0:T(8,128)(2,1)S(1)}, u32[]{:S(2)}, u32[]{:S(2)}) collective-permute-start(bf16[24,3200]{1,0:T(8,128)(2,1)S(1)} %get-tuple-element.10), channel_id=1, source_target_pairs={{0,193},{1,192},{64,129},{65,128},{128,65},{129,64},{192,1},{193,0... | collective-permute-start | bytes 460808 | tf_op jit(solution)/shard_map/ppermute | solution.py:272
  16.8 8.1 %collective-permute-start.12 = (bf16[24,3200]{1,0:T(8,128)(2,1)S(1)}, bf16[24,3200]{1,0:T(8,128)(2,1)S(1)}, u32[]{:S(2)}, u32[]{:S(2)}) collective-permute-start(bf16[24,3200]{1,0:T(8,128)(2,1)S(1)} %add.14), channel_id=1, source_target_pairs={{0,4},{2,6},{4,0},{6,2},{1,5},{3,7},{5,1},{7,3},{8,12},{10,14},{12... | collective-permute-start | bytes 460808 | tf_op jit(solution)/shard_map/ppermute | solution.py:243
  19.8 7.0 %collective-permute-start.11 = (bf16[24,3200]{1,0:T(8,128)(2,1)S(1)}, bf16[24,3200]{1,0:T(8,128)(2,1)S(1)}, u32[]{:S(2)}, u32[]{:S(2)}) collective-permute-start(bf16[24,3200]{1,0:T(8,128)(2,1)S(1)} %add.14), channel_id=1, source_target_pairs={{0,6},{2,0},{4,2},{6,4},{1,7},{3,1},{5,3},{7,5},{8,14},{10,8},{12,... | collective-permute-start | bytes 460808 | tf_op jit(solution)/shard_map/ppermute | solution.py:243
  20.6 6.3 %collective-permute-start.10 = (bf16[24,3200]{1,0:T(8,128)(2,1)S(1)}, bf16[24,3200]{1,0:T(8,128)(2,1)S(1)}, u32[]{:S(2)}, u32[]{:S(2)}) collective-permute-start(bf16[24,3200]{1,0:T(8,128)(2,1)S(1)} %add.14), channel_id=1, source_target_pairs={{0,2},{2,4},{4,6},{6,0},{1,3},{3,5},{5,7},{7,1},{8,10},{10,12},{12... | collective-permute-start | bytes 460808 | tf_op jit(solution)/shard_map/ppermute | solution.py:243
  21.3 8.5 %collective-permute-start.6 = (bf16[16,3200]{1,0:T(8,128)(2,1)S(1)}, bf16[16,3200]{1,0:T(8,128)(2,1)S(1)}, u32[]{:S(2)}, u32[]{:S(2)}) collective-permute-start(bf16[16,3200]{1,0:T(8,128)(2,1)S(1)} %get-tuple-element.8), channel_id=1, source_target_pairs={{0,16},{8,24},{16,0},{24,8},{1,17},{9,25},{17,1},{25,9},{2,18},{10... | collective-permute-start | bytes 307208 | tf_op jit(solution)/shard_map/ppermute | solution.py:243
  24.0 5.7 %collective-permute-start.5 = (bf16[16,3200]{1,0:T(8,128)(2,1)S(1)}, bf16[16,3200]{1,0:T(8,128)(2,1)S(1)}, u32[]{:S(2)}, u32[]{:S(2)}) collective-permute-start(bf16[16,3200]{1,0:T(8,128)(2,1)S(1)} %get-tuple-element.8), channel_id=1, source_target_pairs={{0,24},{8,0},{16,8},{24,16},{1,25},{9,1},{17,9},{25,17},{2,26},{10... | collective-permute-start | bytes 307208 | tf_op jit(solution)/shard_map/ppermute | solution.py:243
  24.9 5.2 %collective-permute-start.4 = (bf16[16,3200]{1,0:T(8,128)(2,1)S(1)}, bf16[16,3200]{1,0:T(8,128)(2,1)S(1)}, u32[]{:S(2)}, u32[]{:S(2)}) collective-permute-start(bf16[16,3200]{1,0:T(8,128)(2,1)S(1)} %get-tuple-element.8), channel_id=1, source_target_pairs={{0,8},{8,16},{16,24},{24,0},{1,9},{9,17},{17,25},{25,1},{2,10},{10... | collective-permute-start | bytes 307208 | tf_op jit(solution)/shard_map/ppermute | solution.py:243
  27.0 16.5 %collective-permute-start.15 = (bf16[4,24,3200]{2,1,0:T(8,128)(2,1)S(1)}, bf16[4,24,3200]{2,1,0:T(8,128)(2,1)S(1)}, u32[]{:S(2)}, u32[]{:S(2)}) collective-permute-start(bf16[4,24,3200]{2,1,0:T(8,128)(2,1)S(1)} %pad_maximum_fusion.refs_9_), channel_id=1, source_target_pairs={{0,8},{8,16},{16,24},{24,0},{1,9},{9,17},{17,25},{25,1},{2,10},{10... | collective-permute-start | bytes 1843208 | tf_op jit(solution)/shard_map/ppermute | solution.py:243
  28.3 15.9 %collective-permute-start.16 = (bf16[4,24,3200]{2,1,0:T(8,128)(2,1)S(1)}, bf16[4,24,3200]{2,1,0:T(8,128)(2,1)S(1)}, u32[]{:S(2)}, u32[]{:S(2)}) collective-permute-start(bf16[4,24,3200]{2,1,0:T(8,128)(2,1)S(1)} %pad_maximum_fusion.refs_9_), channel_id=1, source_target_pairs={{0,24},{8,0},{16,8},{24,16},{1,25},{9,1},{17,9},{25,17},{2,26},{10... | collective-permute-start | bytes 1843208 | tf_op jit(solution)/shard_map/ppermute | solution.py:243
  30.2 16.3 %collective-permute-start.7 = (bf16[4,16,3200]{2,1,0:T(8,128)(2,1)S(1)}, bf16[4,16,3200]{2,1,0:T(8,128)(2,1)S(1)}, u32[]{:S(2)}, u32[]{:S(2)}) collective-permute-start(bf16[4,16,3200]{2,1,0:T(8,128)(2,1)S(1)} %pad_maximum_fusion.1.refs_6_), channel_id=1, source_target_pairs={{0,2},{2,4},{4,6},{6,0},{1,3},{3,5},{5,7},{7,1},{8,10},{10,12},{12... | collective-permute-start | bytes 1228808 | tf_op jit(solution)/shard_map/ppermute | solution.py:243
  31.9 16.4 %collective-permute-start.8 = (bf16[4,16,3200]{2,1,0:T(8,128)(2,1)S(1)}, bf16[4,16,3200]{2,1,0:T(8,128)(2,1)S(1)}, u32[]{:S(2)}, u32[]{:S(2)}) collective-permute-start(bf16[4,16,3200]{2,1,0:T(8,128)(2,1)S(1)} %pad_maximum_fusion.1.refs_6_), channel_id=1, source_target_pairs={{0,6},{2,0},{4,2},{6,4},{1,7},{3,1},{5,3},{7,5},{8,14},{10,8},{12,... | collective-permute-start | bytes 1228808 | tf_op jit(solution)/shard_map/ppermute | solution.py:243
  43.6 42.6 %collective-permute-start.17 = (bf16[2,24,3200]{2,1,0:T(8,128)(2,1)S(1)}, bf16[2,24,3200]{2,1,0:T(8,128)(2,1)S(1)}, u32[]{:S(2)}, u32[]{:S(2)}) collective-permute-start(bf16[2,24,3200]{2,1,0:T(8,128)(2,1)S(1)} %slice.22), channel_id=1, source_target_pairs={{0,8},{8,16},{16,24},{24,0},{1,9},{9,17},{17,25},{25,1},{2,10},{10... | collective-permute-start | bytes 921608 | tf_op jit(solution)/shard_map/ppermute | solution.py:243
  44.2 42.0 %collective-permute-start.18 = (bf16[2,24,3200]{2,1,0:T(8,128)(2,1)S(1)}, bf16[2,24,3200]{2,1,0:T(8,128)(2,1)S(1)}, u32[]{:S(2)}, u32[]{:S(2)}) collective-permute-start(bf16[2,24,3200]{2,1,0:T(8,128)(2,1)S(1)} %slice.23), channel_id=1, source_target_pairs={{0,24},{8,0},{16,8},{24,16},{1,25},{9,1},{17,9},{25,17},{2,26},{10... | collective-permute-start | bytes 921608 | tf_op jit(solution)/shard_map/ppermute | solution.py:243
  46.5 33.1 %collective-permute-start.13 = (bf16[2,16,3200]{2,1,0:T(8,128)(2,1)S(1)}, bf16[2,16,3200]{2,1,0:T(8,128)(2,1)S(1)}, u32[]{:S(2)}, u32[]{:S(2)}) collective-permute-start(bf16[2,16,3200]{2,1,0:T(8,128)(2,1)S(1)} %slice.20), channel_id=1, source_target_pairs={{0,2},{2,4},{4,6},{6,0},{1,3},{3,5},{5,7},{7,1},{8,10},{10,12},{12... | collective-permute-start | bytes 614408 | tf_op jit(solution)/shard_map/ppermute | solution.py:243
  48.4 31.2 %collective-permute-start.14 = (bf16[2,16,3200]{2,1,0:T(8,128)(2,1)S(1)}, bf16[2,16,3200]{2,1,0:T(8,128)(2,1)S(1)}, u32[]{:S(2)}, u32[]{:S(2)}) collective-permute-start(bf16[2,16,3200]{2,1,0:T(8,128)(2,1)S(1)} %slice.21), channel_id=1, source_target_pairs={{0,6},{2,0},{4,2},{6,4},{1,7},{3,1},{5,3},{7,5},{8,14},{10,8},{12,... | collective-permute-start | bytes 614408 | tf_op jit(solution)/shard_map/ppermute | solution.py:243
  50.3 3.1 %collective-permute-start = (s32[1,400]{1,0:T(1,128)S(1)}, s32[1,400]{1,0:T(1,128)S(1)}, u32[]{:S(2)}, u32[]{:S(2)}) collective-permute-start(s32[1,400]{1,0:T(1,128)S(1)} %copy-done.3), channel_id=1, source_target_pairs={{0,32},{32,0},{1,33},{33,1},{2,34},{34,2},{3,35},{35,3},{4,36},{36... | collective-permute-start | bytes 4808 | tf_op jit(solution)/shard_map/ppermute | solution.py:270
  53.4 4.5 %collective-permute-start.1 = (s32[2,400]{1,0:T(2,128)S(1)}, s32[2,400]{1,0:T(2,128)S(1)}, u32[]{:S(2)}, u32[]{:S(2)}) collective-permute-start(s32[2,400]{1,0:T(2,128)S(1)} %pad_add_fusion.refs_0_), channel_id=1, source_target_pairs={{0,64},{64,128},{128,192},{192,0},{1,65},{65,129},{129,193},{193,1... | collective-permute-start | bytes 9608 | tf_op jit(solution)/shard_map/ppermute | solution.py:243
  57.9 3.4 %collective-permute-start.2 = (s32[2,400]{1,0:T(2,128)S(1)}, s32[2,400]{1,0:T(2,128)S(1)}, u32[]{:S(2)}, u32[]{:S(2)}) collective-permute-start(s32[2,400]{1,0:T(2,128)S(1)} %pad_add_fusion.refs_0_), channel_id=1, source_target_pairs={{0,128},{64,192},{128,0},{192,64},{1,129},{65,193},{129,1},{193,65... | collective-permute-start | bytes 9608 | tf_op jit(solution)/shard_map/ppermute | solution.py:243
  61.3 2.5 %collective-permute-start.3 = (s32[2,400]{1,0:T(2,128)S(1)}, s32[2,400]{1,0:T(2,128)S(1)}, u32[]{:S(2)}, u32[]{:S(2)}) collective-permute-start(s32[2,400]{1,0:T(2,128)S(1)} %pad_add_fusion.refs_0_), channel_id=1, source_target_pairs={{0,192},{64,0},{128,64},{192,128},{1,193},{65,1},{129,65},{193,129... | collective-permute-start | bytes 9608 | tf_op jit(solution)/shard_map/ppermute | solution.py:243
  92.7 11.5 %all-to-all-start = ((f32[16,48,128]{2,1,0:T(8,128)}), f32[16,48,128]{2,1,0:T(8,128)S(1)}, u32[]{:S(2)}, u32[]{:S(2)}) async-start(f32[16,48,128]{2,1,0:T(8,128)} %shard_map.39), calls=%async_computation | async-start | bytes 786432 | tf_op jit(solution)/shard_map/all_to_all | solution.py:287
  104.2 10.1 %collective-permute-start.19 = (f32[19,128]{1,0:T(8,128)S(1)}, f32[19,128]{1,0:T(8,128)S(1)}, u32[]{:S(2)}, u32[]{:S(2)}) collective-permute-start(f32[19,128]{1,0:T(8,128)S(1)} %get-tuple-element.12), channel_id=1, source_target_pairs={{0,0},{1,33},{2,66},{3,99},{4,132},{5,165},{6,198},{7,231},{8,8},{... | collective-permute-start | bytes 29192 | tf_op jit(solution)/shard_map/ppermute | solution.py:290
  108.0 7.2 %collective-permute-start.20 = (f32[19,128]{1,0:T(8,128)S(1)}, f32[19,128]{1,0:T(8,128)S(1)}, u32[]{:S(2)}, u32[]{:S(2)}) collective-permute-start(f32[19,128]{1,0:T(8,128)S(1)} %get-tuple-element.11), channel_id=1, source_target_pairs={{0,33},{1,0},{2,99},{3,66},{4,165},{5,132},{6,231},{7,198},{8,41},... | collective-permute-start | bytes 29192 | tf_op jit(solution)/shard_map/ppermute | solution.py:291
where the time goes:
time: 117 us; the launch traced here: 116 us
  starting transfers between devices  43.9 us (38%)
  waiting for transfers between devices  38.9 us (33%)
  Pallas kernels  29.5 us (25%)
  local copies, waits for them, and re-layouts  2.46 us (2%)
    ppermute x17, waiting for transfers between devices, shifted(): return lax.ppermute(array, axis, [(i, (i + by) % n) for i in range(n)])  22 us
    ppermute x17, starting transfers between devices, shifted(): return lax.ppermute(array, axis, [(i, (i + by) % n) for i in range(n)])  21.5 us
    pallas_call x3, Pallas kernels, windows(): pl.pallas_call(functools.partial(window_kernel, len(parts), spots, done),...  21.2 us
    all_to_all x1, waiting for transfers between devices, in_plane(): arrived = lax.all_to_all(dealt, ('x', 'y'), 0, 0, tiled=True).sum(axis=0)  7.92 us
    pallas_call x1, Pallas kernels, genes(): pl.pallas_call(gene_kernel, out_shape=jax.ShapeDtypeStruct((COHORTS, GENE...  7.69 us
    ppermute x1, waiting for transfers between devices, in_plane(): across = lax.ppermute(theirs, ('z_lo', 'z_hi'), pairs)  7.28 us
    ppermute x1, starting transfers between devices, in_plane(): across = lax.ppermute(theirs, ('z_lo', 'z_hi'), pairs)  6.49 us
    ppermute x1, starting transfers between devices, in_plane(): lax.ppermute(lax.dynamic_index_in_dim(arrived, 1 - z_hi, 0, False), ALL_A...  6.35 us
  transfers between devices with their start and end apart: 22, of which 11 were waited for; matrix products, arithmetic and copies ran while one was open for 0% of the time, Pallas kernels for 19%

commit v1 on v0

--- a/solution.py
+++ b/solution.py
@@ -66,8 +66,18 @@
     return [(ref, row) for ref in refs for row in range(2)]
 
 
+def brought(lists, here, ready):
+    return [pltpu.make_async_copy(a, b, ready.at[i]) for i, (a, b) in enumerate(zip(lists, here, strict=True))]
+
+
+def list_scratch():
+    return [pltpu.SMEM((2, SAMPLES), jnp.int32)] * 4 + [pltpu.SemaphoreType.DMA((4,))]
+
+
 def gene_kernel(*refs):
-    lists, (x_hbm, z_ref, x_ref, turned, even, odd, arrive) = refs[:4], refs[4:]
+    lists, (x_hbm, z_ref, x_ref, turned, even, odd, arrive, *here, ready) = refs[:4], refs[4:]
+    for copy in brought(lists, here, ready):
+        copy.start()
 
     def fetch(i):
         lanes = pl.ds(pl.multiple_of(i * CHUNK, LANES), CHUNK)
@@ -96,14 +106,16 @@
             z = jnp.concatenate([z, jnp.zeros((DEPTH - SAMPLES, LANES), F32)], axis=0).astype(BF16)
             z_ref[c, b * LANES : (b + 1) * LANES, :] = z.T
 
-    in_turn(order_of(lists), turned, (even, odd), GENE_BLOCKS, finish)
+    for copy in brought(lists, here, ready):
+        copy.wait()
+    in_turn(order_of(here), turned, (even, odd), GENE_BLOCKS, finish)
 
 
 def genes(lists, x):
     return pl.pallas_call(
         gene_kernel,
         out_shape=jax.ShapeDtypeStruct((COHORTS, GENE_BLOCKS * LANES, DEPTH), BF16),
-        in_specs=[pl.BlockSpec(memory_space=pltpu.SMEM)] * 4 + [pl.BlockSpec(memory_space=pltpu.HBM)],
+        in_specs=[pl.BlockSpec(memory_space=pl.ANY)] * 4 + [pl.BlockSpec(memory_space=pltpu.HBM)],
         out_specs=pl.BlockSpec(memory_space=pltpu.VMEM),
         scratch_shapes=[
             pltpu.VMEM((GENES, POOL), BF16),
@@ -111,6 +123,7 @@
             pltpu.VMEM((GENE_BLOCKS * SHORT, LANES), F32),
             pltpu.VMEM((GENE_BLOCKS * SHORT, LANES), F32),
             pltpu.SemaphoreType.DMA((POOL // CHUNK,)),
+            *list_scratch(),
         ],
         compiler_params=pltpu.CompilerParams(vmem_limit_bytes=26 * 2**20),
         name="genes",
@@ -156,7 +169,9 @@
 def window_kernel(units, spots, done, *refs):
     lists, (module_ref, z_ref), refs = refs[:4], refs[4:6], refs[6:]
     before, parts, refs = refs[: len(done)], refs[len(done) : len(done) + units], refs[len(done) + units :]
-    out_ref, turned, even, odd, zw0, zw1, low, consensus, label, raw = refs
+    out_ref, turned, even, odd, zw0, zw1, low, consensus, label, raw, *here, ready = refs
+    for copy in brought(lists, here, ready):
+        copy.start()
     total = low.shape[1]
     blocks = total // LANES
     strips = [(p, j, r) for p in parts for j in range(p.shape[0]) for r in range(0, p.shape[1], 8)]
@@ -177,7 +192,9 @@
         corr = jnp.dot(z_ref[c], zw[...], preferred_element_type=F32)
         low[...] = jnp.minimum(low[...], corr) if c else corr
 
-    in_turn(order_of(lists), turned, (even, odd), blocks, finish)
+    for copy in brought(lists, here, ready):
+        copy.wait()
+    in_turn(order_of(here), turned, (even, odd), blocks, finish)
 
     base = (1.0 + jnp.maximum(low[...], -1.0)) * 0.5
     square = base * base
@@ -220,7 +237,7 @@
     return pl.pallas_call(
         functools.partial(window_kernel, len(parts), spots, done),
         out_shape=jax.ShapeDtypeStruct(shape, F32),
-        in_specs=[pl.BlockSpec(memory_space=pltpu.SMEM)] * 4
+        in_specs=[pl.BlockSpec(memory_space=pl.ANY)] * 4
         + [pl.BlockSpec(memory_space=pltpu.VMEM)] * (2 + len(sums) + len(parts)),
         out_specs=pl.BlockSpec(memory_space=pltpu.VMEM),
         scratch_shapes=[
@@ -233,6 +250,7 @@
             pltpu.VMEM((GENE_BLOCKS * LANES, total), BF16),
             pltpu.VMEM((1, GENE_BLOCKS * LANES), jnp.int32),
             pltpu.VMEM((total, MODULES), F32),
+            *list_scratch(),
         ],
         compiler_params=pltpu.CompilerParams(vmem_limit_bytes=20 * 2**20),
     )(*lists, module, z, *sums, *parts)
@@ -273,6 +291,8 @@
     lists = [both] + [shifted(both, "z_lo", by) for by in (1, 2, 3)]
 
     near = gathered(own, "x", "y")
+    mine, stack = lax.optimization_barrier((mine, near[0][0]))
+    near[0] = (stack, near[0][1])
     far = gathered(mine + across, "y", "x")
     z = genes(lists, expression)
     module = gene_block.reshape(1, GENES)

time: 117 us -> 118 us (level)
  Pallas kernels: 29.5 us -> 26.8 us
  waiting for transfers between devices: 38.9 us -> 41.1 us
    ppermute x17, waiting for transfers between devices: 22 us -> 24.3 us  [shifted(): return lax.ppermute(array, axis, [(i, (i + by) % n) for i in range(n)])]
    ppermute x17, starting transfers between devices: 21.5 us -> 23.6 us  [shifted(): return lax.ppermute(array, axis, [(i, (i + by) % n) for i in range(n)])]
    pallas_call x3, Pallas kernels: 21.2 us -> 19.2 us  [windows(): pl.pallas_call(functools.partial(window_kernel, len(parts), spots, done),...]
  transfers between devices with their start and end apart: 22 -> 22, of which waited for: 11 -> 11; matrix products, arithmetic and copies ran while one was open for 0% -> 0% of each run, Pallas kernels for 19% -> 18%
where the time goes in v1:
time: 118 us; the launch traced here: 116 us
  starting transfers between devices  44.7 us (38%)
  waiting for transfers between devices  41.1 us (35%)
  Pallas kernels  26.8 us (23%)
  local copies, waits for them, and re-layouts  2.46 us (2%)
    ppermute x17, waiting for transfers between devices, shifted(): return lax.ppermute(array, axis, [(i, (i + by) % n) for i in range(n)])  24.3 us
    ppermute x17, starting transfers between devices, shifted(): return lax.ppermute(array, axis, [(i, (i + by) % n) for i in range(n)])  23.6 us
    pallas_call x3, Pallas kernels, windows(): pl.pallas_call(functools.partial(window_kernel, len(parts), spots, done),...  19.2 us
    all_to_all x1, waiting for transfers between devices, in_plane(): arrived = lax.all_to_all(dealt, ('x', 'y'), 0, 0, tiled=True).sum(axis=0)  7.92 us
    ppermute x1, waiting for transfers between devices, in_plane(): across = lax.ppermute(theirs, ('z_lo', 'z_hi'), pairs)  7.19 us
    pallas_call x1, Pallas kernels, genes(): pl.pallas_call(gene_kernel, out_shape=jax.ShapeDtypeStruct((COHORTS, GENE...  6.99 us
    ppermute x1, starting transfers between devices, in_plane(): lax.ppermute(lax.dynamic_index_in_dim(arrived, 1 - z_hi, 0, False), ALL_A...  5.78 us
    ppermute x1, starting transfers between devices, in_plane(): across = lax.ppermute(theirs, ('z_lo', 'z_hi'), pairs)  5.57 us
  transfers between devices with their start and end apart: 22, of which 11 were waited for; matrix products, arithmetic and copies ran while one was open for 0% of the time, Pallas kernels for 18%

profile of v1, /device:TPU:1, one launch (start us, length us, event | category | flops | bytes accessed | tf_op | source)
XLA Modules:
  0.0 116.1 jit_solution(1412242213257553010)
XLA Ops:
  0.0 2.4 %copy-done = bf16[750,3200]{1,0:T(8,128)(2,1)S(1)} copy-done((bf16[750,3200]{1,0:T(8,128)(2,1)S(1)}, bf16[750,3200]{1,0:T(8,128)(2,1)}, u32[]{:S(2)}) %copy-start) | copy-done | bytes 4800024
  2.4 0.6 pick.1
  3.0 3.7 %collective-permute-start.6 = (bf16[16,3200]{1,0:T(8,128)(2,1)S(1)}, bf16[16,3200]{1,0:T(8,128)(2,1)S(1)}, u32[]{:S(2)}, u32[]{:S(2)}) collective-permute-start(bf16[16,3200]{1,0:T(8,128)(2,1)S(1)} %get-tuple-element.11), channel_id=1, source_target_pairs={{0,16},{8,24},{16,0},{24,8},{1,17},{9,25},{17,1},{25,9},{2,18},{10... | collective-permute-start | bytes 307208 | tf_op jit(solution)/shard_map/ppermute | solution.py:261
  6.7 0.9 collective-permute-start.5
  8.1 5.6 %collective-permute-start.9 = (bf16[24,3200]{1,0:T(8,128)(2,1)S(1)}, bf16[24,3200]{1,0:T(8,128)(2,1)S(1)}, u32[]{:S(2)}, u32[]{:S(2)}) collective-permute-start(bf16[24,3200]{1,0:T(8,128)(2,1)S(1)} %get-tuple-element.14), channel_id=1, source_target_pairs={{0,193},{1,192},{64,129},{65,128},{128,65},{129,64},{192,1},{193,0... | collective-permute-start | bytes 460808 | tf_op jit(solution)/shard_map/ppermute | solution.py:290
  13.8 7.2 %collective-permute-done.9 = bf16[24,3200]{1,0:T(8,128)(2,1)S(1)} collective-permute-done((bf16[24,3200]{1,0:T(8,128)(2,1)S(1)}, bf16[24,3200]{1,0:T(8,128)(2,1)S(1)}, u32[]{:S(2)}, u32[]{:S(2)}) %collective-permute-start.9) | collective-permute-done | bytes 153632 | tf_op jit(solution)/shard_map/ppermute | solution.py:290
  21.0 3.0 %collective-permute-start.12 = (bf16[24,3200]{1,0:T(8,128)(2,1)S(1)}, bf16[24,3200]{1,0:T(8,128)(2,1)S(1)}, u32[]{:S(2)}, u32[]{:S(2)}) collective-permute-start(bf16[24,3200]{1,0:T(8,128)(2,1)S(1)} %add.14), channel_id=1, source_target_pairs={{0,4},{2,6},{4,0},{6,2},{1,5},{3,7},{5,1},{7,3},{8,12},{10,14},{12... | collective-permute-start | bytes 460808 | tf_op jit(solution)/shard_map/ppermute | solution.py:261
  24.0 0.8 collective-permute-start.11
  24.8 0.7 collective-permute-start.10
  25.5 1.7 %collective-permute-done.12 = bf16[24,3200]{1,0:T(8,128)(2,1)S(1)} collective-permute-done((bf16[24,3200]{1,0:T(8,128)(2,1)S(1)}, bf16[24,3200]{1,0:T(8,128)(2,1)S(1)}, u32[]{:S(2)}, u32[]{:S(2)}) %collective-permute-start.12) | collective-permute-done | bytes 153632 | tf_op jit(solution)/shard_map/ppermute | solution.py:261
  27.2 3.8 %collective-permute-done.11 = bf16[24,3200]{1,0:T(8,128)(2,1)S(1)} collective-permute-done((bf16[24,3200]{1,0:T(8,128)(2,1)S(1)}, bf16[24,3200]{1,0:T(8,128)(2,1)S(1)}, u32[]{:S(2)}, u32[]{:S(2)}) %collective-permute-start.11) | collective-permute-done | bytes 153632 | tf_op jit(solution)/shard_map/ppermute | solution.py:261
  31.6 2.3 %collective-permute-start.16 = (bf16[4,24,3200]{2,1,0:T(8,128)(2,1)S(1)}, bf16[4,24,3200]{2,1,0:T(8,128)(2,1)S(1)}, u32[]{:S(2)}, u32[]{:S(2)}) collective-permute-start(bf16[4,24,3200]{2,1,0:T(8,128)(2,1)S(1)} %pad_maximum_fusion.refs_9_), channel_id=1, source_target_pairs={{0,24},{8,0},{16,8},{24,16},{1,25},{9,1},{17,9},{25,17},{2,26},{10... | collective-permute-start | bytes 1843208 | tf_op jit(solution)/shard_map/ppermute | solution.py:261
  33.9 2.0 %collective-permute-start.7 = (bf16[4,16,3200]{2,1,0:T(8,128)(2,1)S(1)}, bf16[4,16,3200]{2,1,0:T(8,128)(2,1)S(1)}, u32[]{:S(2)}, u32[]{:S(2)}) collective-permute-start(bf16[4,16,3200]{2,1,0:T(8,128)(2,1)S(1)} %pad_maximum_fusion.1.refs_6_), channel_id=1, source_target_pairs={{0,2},{2,4},{4,6},{6,0},{1,3},{3,5},{5,7},{7,1},{8,10},{10,12},{12... | collective-permute-start | bytes 1228808 | tf_op jit(solution)/shard_map/ppermute | solution.py:261
  35.9 1.3 %collective-permute-start.8 = (bf16[4,16,3200]{2,1,0:T(8,128)(2,1)S(1)}, bf16[4,16,3200]{2,1,0:T(8,128)(2,1)S(1)}, u32[]{:S(2)}, u32[]{:S(2)}) collective-permute-start(bf16[4,16,3200]{2,1,0:T(8,128)(2,1)S(1)} %pad_maximum_fusion.1.refs_6_), channel_id=1, source_target_pairs={{0,6},{2,0},{4,2},{6,4},{1,7},{3,1},{5,3},{7,5},{8,14},{10,8},{12,... | collective-permute-start | bytes 1228808 | tf_op jit(solution)/shard_map/ppermute | solution.py:261
  37.3 8.8 %collective-permute-done.15.refs_8_ = bf16[4,24,3200]{2,1,0:T(8,128)(2,1)S(1)} collective-permute-done((bf16[4,24,3200]{2,1,0:T(8,128)(2,1)S(1)}, bf16[4,24,3200]{2,1,0:T(8,128)(2,1)S(1)}, u32[]{:S(2)}, u32[]{:S(2)}) %collective-permute-start.15) | collective-permute-done | bytes 614432 | tf_op jit(solution)/shard_map/ppermute | solution.py:261
  46.2 2.7 %collective-permute-start.18 = (bf16[2,24,3200]{2,1,0:T(8,128)(2,1)S(1)}, bf16[2,24,3200]{2,1,0:T(8,128)(2,1)S(1)}, u32[]{:S(2)}, u32[]{:S(2)}) collective-permute-start(bf16[2,24,3200]{2,1,0:T(8,128)(2,1)S(1)} %slice.23), channel_id=1, source_target_pairs={{0,24},{8,0},{16,8},{24,16},{1,25},{9,1},{17,9},{25,17},{2,26},{10... | collective-permute-start | bytes 921608 | tf_op jit(solution)/shard_map/ppermute | solution.py:261
  49.0 3.3 %collective-permute-start.13 = (bf16[2,16,3200]{2,1,0:T(8,128)(2,1)S(1)}, bf16[2,16,3200]{2,1,0:T(8,128)(2,1)S(1)}, u32[]{:S(2)}, u32[]{:S(2)}) collective-permute-start(bf16[2,16,3200]{2,1,0:T(8,128)(2,1)S(1)} %slice.20), channel_id=1, source_target_pairs={{0,2},{2,4},{4,6},{6,0},{1,3},{3,5},{5,7},{7,1},{8,10},{10,12},{12... | collective-permute-start | bytes 614408 | tf_op jit(solution)/shard_map/ppermute | solution.py:261
  52.3 1.5 %collective-permute-start.14 = (bf16[2,16,3200]{2,1,0:T(8,128)(2,1)S(1)}, bf16[2,16,3200]{2,1,0:T(8,128)(2,1)S(1)}, u32[]{:S(2)}, u32[]{:S(2)}) collective-permute-start(bf16[2,16,3200]{2,1,0:T(8,128)(2,1)S(1)} %slice.21), channel_id=1, source_target_pairs={{0,6},{2,0},{4,2},{6,4},{1,7},{3,1},{5,3},{7,5},{8,14},{10,8},{12,... | collective-permute-start | bytes 614408 | tf_op jit(solution)/shard_map/ppermute | solution.py:261
  53.7 2.3 %collective-permute-start = (s32[1,400]{1,0:T(1,128)S(1)}, s32[1,400]{1,0:T(1,128)S(1)}, u32[]{:S(2)}, u32[]{:S(2)}) collective-permute-start(s32[1,400]{1,0:T(1,128)S(1)} %copy-done.3), channel_id=1, source_target_pairs={{0,32},{32,0},{1,33},{33,1},{2,34},{34,2},{3,35},{35,3},{4,36},{36... | collective-permute-start | bytes 4808 | tf_op jit(solution)/shard_map/ppermute | solution.py:288
  56.0 0.8 collective-permute-done
  57.1 4.2 %collective-permute-done.1.refs_1_ = s32[2,400]{1,0:T(2,128)S(1)} collective-permute-done((s32[2,400]{1,0:T(2,128)S(1)}, s32[2,400]{1,0:T(2,128)S(1)}, u32[]{:S(2)}, u32[]{:S(2)}) %collective-permute-start.1) | collective-permute-done | bytes 3232 | tf_op jit(solution)/shard_map/ppermute | solution.py:261
  61.4 3.4 %collective-permute-done.2.refs_2_ = s32[2,400]{1,0:T(2,128)S(1)} collective-permute-done((s32[2,400]{1,0:T(2,128)S(1)}, s32[2,400]{1,0:T(2,128)S(1)}, u32[]{:S(2)}, u32[]{:S(2)}) %collective-permute-start.2) | collective-permute-done | bytes 3232 | tf_op jit(solution)/shard_map/ppermute | solution.py:261
  64.8 2.4 %collective-permute-done.3.refs_3_ = s32[2,400]{1,0:T(2,128)S(1)} collective-permute-done((s32[2,400]{1,0:T(2,128)S(1)}, s32[2,400]{1,0:T(2,128)S(1)}, u32[]{:S(2)}, u32[]{:S(2)}) %collective-permute-start.3) | collective-permute-done | bytes 3232 | tf_op jit(solution)/shard_map/ppermute | solution.py:261
  67.2 7.0 %genes.1.refs_5_ = bf16[8,768,512]{2,1,0:T(8,128)(2,1)S(1)} custom-call(s32[2,400]{1,0:T(2,128)S(1)} %pad_add_fusion.refs_0_, s32[2,400]{1,0:T(2,128)S(1)} %collective-permute-done.1.refs_1_, s32[2,400]{1,0:T(2,128)S(1)} %collective-permute-done.2.refs_2_, s32[2,400]{1,0:T(2,128)S(1)} %collective-permute-done.3.refs_3_, bf16[750,3200]{1,0:T(8,128)(2,1)S(1)} %copy-done.1), custom_call_target="tpu_custom_call" | custom-call | tf_op jit(solution)/shard_map/genes/pallas_call | solution.py:115
  74.2 7.4 %shard_map.37.refs_6_ = f32[384,128]{1,0:T(8,128)S(1)} custom-call(s32[2,400]{1,0:T(2,128)S(1)} %pad_add_fusion.refs_0_, s32[2,400]{1,0:T(2,128)S(1)} %collective-permute-done.1.refs_1_, s32[2,400]{1,0:T(2,128)S(1)} %collective-permute-done.2.refs_2_, s32[2,400]{1,0:T(2,128)S(1)} %collective-permute-done.3.refs_3_, s32[1,750]{1,0:T(1,128)S(1)} %reshape.6.refs_4_, ...), custom_call_target="tpu_custom_call" | custom-call | tf_op jit(solution)/shard_map/pallas_call | solution.py:237
  81.7 5.9 %shard_map.38.refs_7_ = f32[256,128]{1,0:T(8,128)S(1)} custom-call(s32[2,400]{1,0:T(2,128)S(1)} %pad_add_fusion.refs_0_, s32[2,400]{1,0:T(2,128)S(1)} %collective-permute-done.1.refs_1_, s32[2,400]{1,0:T(2,128)S(1)} %collective-permute-done.2.refs_2_, s32[2,400]{1,0:T(2,128)S(1)} %collective-permute-done.3.refs_3_, s32[1,750]{1,0:T(1,128)S(1)} %reshape.6.refs_4_, ...), custom_call_target="tpu_custom_call" | custom-call | tf_op jit(solution)/shard_map/pallas_call | solution.py:237
  87.6 5.8 %shard_map.39 = f32[16,48,128]{2,1,0:T(8,128)} custom-call(s32[2,400]{1,0:T(2,128)S(1)} %pad_add_fusion.refs_0_, s32[2,400]{1,0:T(2,128)S(1)} %collective-permute-done.1.refs_1_, s32[2,400]{1,0:T(2,128)S(1)} %collective-permute-done.2.refs_2_, s32[2,400]{1,0:T(2,128)S(1)} %collective-permute-done.3.refs_3_, s32[1,750]{1,0:T(1,128)S(1)} %reshape.6.refs_4_, ...), custom_call_target="tpu_custom_call" | custom-call | tf_op jit(solution)/shard_map/pallas_call | solution.py:237
  93.5 3.6 %all-to-all-start = ((f32[16,48,128]{2,1,0:T(8,128)}), f32[16,48,128]{2,1,0:T(8,128)S(1)}, u32[]{:S(2)}, u32[]{:S(2)}) async-start(f32[16,48,128]{2,1,0:T(8,128)} %shard_map.39), calls=%async_computation | async-start | bytes 786432 | tf_op jit(solution)/shard_map/all_to_all | solution.py:307
  97.0 7.9 %all-to-all-done = f32[16,48,128]{2,1,0:T(8,128)S(1)} async-done(((f32[16,48,128]{2,1,0:T(8,128)}), f32[16,48,128]{2,1,0:T(8,128)S(1)}, u32[]{:S(2)}, u32[]{:S(2)}) %all-to-all-start) | async-done | bytes 393248 | tf_op jit(solution)/shard_map/all_to_all | solution.py:307
  105.0 3.8 %collective-permute-start.19 = (f32[19,128]{1,0:T(8,128)S(1)}, f32[19,128]{1,0:T(8,128)S(1)}, u32[]{:S(2)}, u32[]{:S(2)}) collective-permute-start(f32[19,128]{1,0:T(8,128)S(1)} %get-tuple-element.16), channel_id=1, source_target_pairs={{0,0},{1,33},{2,66},{3,99},{4,132},{5,165},{6,198},{7,231},{8,8},{... | collective-permute-start | bytes 29192 | tf_op jit(solution)/shard_map/ppermute | solution.py:310
  108.9 5.8 %collective-permute-start.20 = (f32[19,128]{1,0:T(8,128)S(1)}, f32[19,128]{1,0:T(8,128)S(1)}, u32[]{:S(2)}, u32[]{:S(2)}) collective-permute-start(f32[19,128]{1,0:T(8,128)S(1)} %get-tuple-element.15), channel_id=1, source_target_pairs={{0,33},{1,0},{2,99},{3,66},{4,165},{5,132},{6,231},{7,198},{8,41},... | collective-permute-start | bytes 29192 | tf_op jit(solution)/shard_map/ppermute | solution.py:311
  114.6 0.8 collective-permute-done.20
  (37 shorter events, 2.5 us)
Async XLA Ops:
  0.0 2.4 %copy-start = (bf16[750,3200]{1,0:T(8,128)(2,1)S(1)}, bf16[750,3200]{1,0:T(8,128)(2,1)}, u32[]{:S(2)}) copy-start(bf16[750,3200]{1,0:T(8,128)(2,1)} %x_hbm.1) | copy-start | bytes 14400004
  2.4 51.4 %copy-start.3 = (s32[1,400]{1,0:T(1,128)S(1)}, s32[1,400]{1,0:T(1,128)}, u32[]{:S(2)}) copy-start(s32[1,400]{1,0:T(1,128)} %param.4) | copy-start | bytes 4804
  2.4 62.5 %copy-start.2 = (s32[750]{0:T(1024)S(1)}, s32[750]{0:T(1024)}, u32[]{:S(2)}) copy-start(s32[750]{0:T(1024)} %param.5) | copy-start | bytes 9004
  2.4 64.8 %copy-start.1 = (bf16[750,3200]{1,0:T(8,128)(2,1)S(1)}, bf16[750,3200]{1,0:T(8,128)(2,1)}, u32[]{:S(2)}) copy-start(bf16[750,3200]{1,0:T(8,128)(2,1)} %x_hbm.1) | copy-start | bytes 14400004
  3.0 10.7 %collective-permute-start.6 = (bf16[16,3200]{1,0:T(8,128)(2,1)S(1)}, bf16[16,3200]{1,0:T(8,128)(2,1)S(1)}, u32[]{:S(2)}, u32[]{:S(2)}) collective-permute-start(bf16[16,3200]{1,0:T(8,128)(2,1)S(1)} %get-tuple-element.11), channel_id=1, source_target_pairs={{0,16},{8,24},{16,0},{24,8},{1,17},{9,25},{17,1},{25,9},{2,18},{10... | collective-permute-start | bytes 307208 | tf_op jit(solution)/shard_map/ppermute | solution.py:261
  6.7 7.0 %collective-permute-start.5 = (bf16[16,3200]{1,0:T(8,128)(2,1)S(1)}, bf16[16,3200]{1,0:T(8,128)(2,1)S(1)}, u32[]{:S(2)}, u32[]{:S(2)}) collective-permute-start(bf16[16,3200]{1,0:T(8,128)(2,1)S(1)} %get-tuple-element.11), channel_id=1, source_target_pairs={{0,24},{8,0},{16,8},{24,16},{1,25},{9,1},{17,9},{25,17},{2,26},{10... | collective-permute-start | bytes 307208 | tf_op jit(solution)/shard_map/ppermute | solution.py:261
  7.5 6.2 %collective-permute-start.4 = (bf16[16,3200]{1,0:T(8,128)(2,1)S(1)}, bf16[16,3200]{1,0:T(8,128)(2,1)S(1)}, u32[]{:S(2)}, u32[]{:S(2)}) collective-permute-start(bf16[16,3200]{1,0:T(8,128)(2,1)S(1)} %get-tuple-element.11), channel_id=1, source_target_pairs={{0,8},{8,16},{16,24},{24,0},{1,9},{9,17},{17,25},{25,1},{2,10},{10... | collective-permute-start | bytes 307208 | tf_op jit(solution)/shard_map/ppermute | solution.py:261
  8.1 12.8 %collective-permute-start.9 = (bf16[24,3200]{1,0:T(8,128)(2,1)S(1)}, bf16[24,3200]{1,0:T(8,128)(2,1)S(1)}, u32[]{:S(2)}, u32[]{:S(2)}) collective-permute-start(bf16[24,3200]{1,0:T(8,128)(2,1)S(1)} %get-tuple-element.14), channel_id=1, source_target_pairs={{0,193},{1,192},{64,129},{65,128},{128,65},{129,64},{192,1},{193,0... | collective-permute-start | bytes 460808 | tf_op jit(solution)/shard_map/ppermute | solution.py:290
  21.0 6.2 %collective-permute-start.12 = (bf16[24,3200]{1,0:T(8,128)(2,1)S(1)}, bf16[24,3200]{1,0:T(8,128)(2,1)S(1)}, u32[]{:S(2)}, u32[]{:S(2)}) collective-permute-start(bf16[24,3200]{1,0:T(8,128)(2,1)S(1)} %add.14), channel_id=1, source_target_pairs={{0,4},{2,6},{4,0},{6,2},{1,5},{3,7},{5,1},{7,3},{8,12},{10,14},{12... | collective-permute-start | bytes 460808 | tf_op jit(solution)/shard_map/ppermute | solution.py:261
  24.0 7.0 %collective-permute-start.11 = (bf16[24,3200]{1,0:T(8,128)(2,1)S(1)}, bf16[24,3200]{1,0:T(8,128)(2,1)S(1)}, u32[]{:S(2)}, u32[]{:S(2)}) collective-permute-start(bf16[24,3200]{1,0:T(8,128)(2,1)S(1)} %add.14), channel_id=1, source_target_pairs={{0,6},{2,0},{4,2},{6,4},{1,7},{3,1},{5,3},{7,5},{8,14},{10,8},{12,... | collective-permute-start | bytes 460808 | tf_op jit(solution)/shard_map/ppermute | solution.py:261
  24.8 6.3 %collective-permute-start.10 = (bf16[24,3200]{1,0:T(8,128)(2,1)S(1)}, bf16[24,3200]{1,0:T(8,128)(2,1)S(1)}, u32[]{:S(2)}, u32[]{:S(2)}) collective-permute-start(bf16[24,3200]{1,0:T(8,128)(2,1)S(1)} %add.14), channel_id=1, source_target_pairs={{0,2},{2,4},{4,6},{6,0},{1,3},{3,5},{5,7},{7,1},{8,10},{10,12},{12... | collective-permute-start | bytes 460808 | tf_op jit(solution)/shard_map/ppermute | solution.py:261
  31.2 14.9 %collective-permute-start.15 = (bf16[4,24,3200]{2,1,0:T(8,128)(2,1)S(1)}, bf16[4,24,3200]{2,1,0:T(8,128)(2,1)S(1)}, u32[]{:S(2)}, u32[]{:S(2)}) collective-permute-start(bf16[4,24,3200]{2,1,0:T(8,128)(2,1)S(1)} %pad_maximum_fusion.refs_9_), channel_id=1, source_target_pairs={{0,8},{8,16},{16,24},{24,0},{1,9},{9,17},{17,25},{25,1},{2,10},{10... | collective-permute-start | bytes 1843208 | tf_op jit(solution)/shard_map/ppermute | solution.py:261
  31.6 14.6 %collective-permute-start.16 = (bf16[4,24,3200]{2,1,0:T(8,128)(2,1)S(1)}, bf16[4,24,3200]{2,1,0:T(8,128)(2,1)S(1)}, u32[]{:S(2)}, u32[]{:S(2)}) collective-permute-start(bf16[4,24,3200]{2,1,0:T(8,128)(2,1)S(1)} %pad_maximum_fusion.refs_9_), channel_id=1, source_target_pairs={{0,24},{8,0},{16,8},{24,16},{1,25},{9,1},{17,9},{25,17},{2,26},{10... | collective-permute-start | bytes 1843208 | tf_op jit(solution)/shard_map/ppermute | solution.py:261
  33.9 15.0 %collective-permute-start.7 = (bf16[4,16,3200]{2,1,0:T(8,128)(2,1)S(1)}, bf16[4,16,3200]{2,1,0:T(8,128)(2,1)S(1)}, u32[]{:S(2)}, u32[]{:S(2)}) collective-permute-start(bf16[4,16,3200]{2,1,0:T(8,128)(2,1)S(1)} %pad_maximum_fusion.1.refs_6_), channel_id=1, source_target_pairs={{0,2},{2,4},{4,6},{6,0},{1,3},{3,5},{5,7},{7,1},{8,10},{10,12},{12... | collective-permute-start | bytes 1228808 | tf_op jit(solution)/shard_map/ppermute | solution.py:261
  35.9 16.3 %collective-permute-start.8 = (bf16[4,16,3200]{2,1,0:T(8,128)(2,1)S(1)}, bf16[4,16,3200]{2,1,0:T(8,128)(2,1)S(1)}, u32[]{:S(2)}, u32[]{:S(2)}) collective-permute-start(bf16[4,16,3200]{2,1,0:T(8,128)(2,1)S(1)} %pad_maximum_fusion.1.refs_6_), channel_id=1, source_target_pairs={{0,6},{2,0},{4,2},{6,4},{1,7},{3,1},{5,3},{7,5},{8,14},{10,8},{12,... | collective-permute-start | bytes 1228808 | tf_op jit(solution)/shard_map/ppermute | solution.py:261
  46.1 41.5 %collective-permute-start.17 = (bf16[2,24,3200]{2,1,0:T(8,128)(2,1)S(1)}, bf16[2,24,3200]{2,1,0:T(8,128)(2,1)S(1)}, u32[]{:S(2)}, u32[]{:S(2)}) collective-permute-start(bf16[2,24,3200]{2,1,0:T(8,128)(2,1)S(1)} %slice.22), channel_id=1, source_target_pairs={{0,8},{8,16},{16,24},{24,0},{1,9},{9,17},{17,25},{25,1},{2,10},{10... | collective-permute-start | bytes 921608 | tf_op jit(solution)/shard_map/ppermute | solution.py:261
  46.2 41.4 %collective-permute-start.18 = (bf16[2,24,3200]{2,1,0:T(8,128)(2,1)S(1)}, bf16[2,24,3200]{2,1,0:T(8,128)(2,1)S(1)}, u32[]{:S(2)}, u32[]{:S(2)}) collective-permute-start(bf16[2,24,3200]{2,1,0:T(8,128)(2,1)S(1)} %slice.23), channel_id=1, source_target_pairs={{0,24},{8,0},{16,8},{24,16},{1,25},{9,1},{17,9},{25,17},{2,26},{10... | collective-permute-start | bytes 921608 | tf_op jit(solution)/shard_map/ppermute | solution.py:261
  49.0 32.7 %collective-permute-start.13 = (bf16[2,16,3200]{2,1,0:T(8,128)(2,1)S(1)}, bf16[2,16,3200]{2,1,0:T(8,128)(2,1)S(1)}, u32[]{:S(2)}, u32[]{:S(2)}) collective-permute-start(bf16[2,16,3200]{2,1,0:T(8,128)(2,1)S(1)} %slice.20), channel_id=1, source_target_pairs={{0,2},{2,4},{4,6},{6,0},{1,3},{3,5},{5,7},{7,1},{8,10},{10,12},{12... | collective-permute-start | bytes 614408 | tf_op jit(solution)/shard_map/ppermute | solution.py:261
  52.3 29.4 %collective-permute-start.14 = (bf16[2,16,3200]{2,1,0:T(8,128)(2,1)S(1)}, bf16[2,16,3200]{2,1,0:T(8,128)(2,1)S(1)}, u32[]{:S(2)}, u32[]{:S(2)}) collective-permute-start(bf16[2,16,3200]{2,1,0:T(8,128)(2,1)S(1)} %slice.21), channel_id=1, source_target_pairs={{0,6},{2,0},{4,2},{6,4},{1,7},{3,1},{5,3},{7,5},{8,14},{10,8},{12,... | collective-permute-start | bytes 614408 | tf_op jit(solution)/shard_map/ppermute | solution.py:261
  53.7 3.1 %collective-permute-start = (s32[1,400]{1,0:T(1,128)S(1)}, s32[1,400]{1,0:T(1,128)S(1)}, u32[]{:S(2)}, u32[]{:S(2)}) collective-permute-start(s32[1,400]{1,0:T(1,128)S(1)} %copy-done.3), channel_id=1, source_target_pairs={{0,32},{32,0},{1,33},{33,1},{2,34},{34,2},{3,35},{35,3},{4,36},{36... | collective-permute-start | bytes 4808 | tf_op jit(solution)/shard_map/ppermute | solution.py:288
  56.9 4.5 %collective-permute-start.1 = (s32[2,400]{1,0:T(2,128)S(1)}, s32[2,400]{1,0:T(2,128)S(1)}, u32[]{:S(2)}, u32[]{:S(2)}) collective-permute-start(s32[2,400]{1,0:T(2,128)S(1)} %pad_add_fusion.refs_0_), channel_id=1, source_target_pairs={{0,64},{64,128},{128,192},{192,0},{1,65},{65,129},{129,193},{193,1... | collective-permute-start | bytes 9608 | tf_op jit(solution)/shard_map/ppermute | solution.py:261
  61.4 3.4 %collective-permute-start.2 = (s32[2,400]{1,0:T(2,128)S(1)}, s32[2,400]{1,0:T(2,128)S(1)}, u32[]{:S(2)}, u32[]{:S(2)}) collective-permute-start(s32[2,400]{1,0:T(2,128)S(1)} %pad_add_fusion.refs_0_), channel_id=1, source_target_pairs={{0,128},{64,192},{128,0},{192,64},{1,129},{65,193},{129,1},{193,65... | collective-permute-start | bytes 9608 | tf_op jit(solution)/shard_map/ppermute | solution.py:261
  64.7 2.5 %collective-permute-start.3 = (s32[2,400]{1,0:T(2,128)S(1)}, s32[2,400]{1,0:T(2,128)S(1)}, u32[]{:S(2)}, u32[]{:S(2)}) collective-permute-start(s32[2,400]{1,0:T(2,128)S(1)} %pad_add_fusion.refs_0_), channel_id=1, source_target_pairs={{0,192},{64,0},{128,64},{192,128},{1,193},{65,1},{129,65},{193,129... | collective-permute-start | bytes 9608 | tf_op jit(solution)/shard_map/ppermute | solution.py:261
  93.5 11.5 %all-to-all-start = ((f32[16,48,128]{2,1,0:T(8,128)}), f32[16,48,128]{2,1,0:T(8,128)S(1)}, u32[]{:S(2)}, u32[]{:S(2)}) async-start(f32[16,48,128]{2,1,0:T(8,128)} %shard_map.39), calls=%async_computation | async-start | bytes 786432 | tf_op jit(solution)/shard_map/all_to_all | solution.py:307
  105.0 9.6 %collective-permute-start.19 = (f32[19,128]{1,0:T(8,128)S(1)}, f32[19,128]{1,0:T(8,128)S(1)}, u32[]{:S(2)}, u32[]{:S(2)}) collective-permute-start(f32[19,128]{1,0:T(8,128)S(1)} %get-tuple-element.16), channel_id=1, source_target_pairs={{0,0},{1,33},{2,66},{3,99},{4,132},{5,165},{6,198},{7,231},{8,8},{... | collective-permute-start | bytes 29192 | tf_op jit(solution)/shard_map/ppermute | solution.py:310
  108.9 6.6 %collective-permute-start.20 = (f32[19,128]{1,0:T(8,128)S(1)}, f32[19,128]{1,0:T(8,128)S(1)}, u32[]{:S(2)}, u32[]{:S(2)}) collective-permute-start(f32[19,128]{1,0:T(8,128)S(1)} %get-tuple-element.15), channel_id=1, source_target_pairs={{0,33},{1,0},{2,99},{3,66},{4,165},{5,132},{6,231},{7,198},{8,41},... | collective-permute-start | bytes 29192 | tf_op jit(solution)/shard_map/ppermute | solution.py:311
